TPU v7x, 256 devices: a whole 4x4x8 slice. The times are simulated.
256 devices in a mesh: row: 16 (over y, x), col: 8 (over z), rep: 2 (over core).
Axes of the slice: x: 4, y: 4, z: 8, core: 2. Of those that a mesh axis runs over, the one named last changes fastest.
Arguments:
- patches: bfloat16 [2, 512, 6144], P('rep', 'col', 'row'), may hold values from -6 to 6
- cotangent: bfloat16 [2, 512, 6144], P('rep', 'col', 'row'), may hold values from -6 to 6
- w_in: bfloat16 [6144, 24576], P('row', 'col'), may hold values from -0.078125 to 0.078125
- w_out: bfloat16 [24576, 6144], P('col', 'row'), may hold values from -0.0390625 to 0.0390625
- moment_in: bfloat16 [2, 6144, 24576], P('rep', 'row', 'col'), may hold values from -2 to 2
- moment_out: bfloat16 [2, 24576, 6144], P('rep', 'col', 'row'), may hold values from -2 to 2
Outputs:
- mixed: bfloat16 [2, 512, 6144], P('rep', 'col', 'row')
- tally_in: bfloat16 [6144, 24576], P('row', 'col')
- tally_out: bfloat16 [24576, 6144], P('col', 'row')
All inputs are finite; a program needn't handle non-finite values.
Results may differ from a plain program's by a relative error of at most 0.0055.
Values may be sent and summed in bfloat16 or wider, within the bound.
A program may use at most 128 MiB of HBM per device.

v0:
```python
import math
import jax
import jax.numpy as jnp
from jax import lax
from jax.sharding import PartitionSpec as P

momentum_decay = 0.9
vote_scale = 0.3


def joined_along(blocks, dim):
    blocks = jnp.moveaxis(blocks, 0, dim)
    lengths = blocks.shape
    return blocks.reshape(*lengths[:dim], lengths[dim] * lengths[dim + 1], *lengths[dim + 2 :])


def sent_to_all(value, axis):
    copies = jnp.broadcast_to(value, (lax.axis_size(axis), *value.shape))
    return lax.all_to_all(copies, axis, split_axis=0, concat_axis=0, tiled=True)


def gather_directly(value, axis, dim):
    return joined_along(sent_to_all(value, axis), dim)


def cut_along(value, dim, peers):
    before, after = (value.shape[:dim], value.shape[dim + 1 :])
    return jnp.moveaxis(value.reshape(*before, peers, -1, *after), dim, 0)


def sum_at_owner(value, axis, dim):
    blocks = cut_along(value, dim, lax.axis_size(axis))
    arrived = lax.all_to_all(blocks, axis, split_axis=0, concat_axis=0, tiled=True)
    return arrived.sum(axis=0)


def gelu_value(pre):
    return 0.5 * pre * (1.0 + lax.erf(pre * (1.0 / math.sqrt(2.0))))


def gelu_slope(pre):
    return 0.5 * (1.0 + lax.erf(pre * (1.0 / math.sqrt(2.0)))) + pre * jnp.exp(-0.5 * pre * pre) * (
        1.0 / math.sqrt(2.0 * math.pi)
    )


def shards(patches, cotangent, w_in, w_out, moment_in, moment_out):
    inputs = gather_directly(patches[0], "col", 0)
    total_rows = inputs.shape[0]
    norm_factor = 1.0 / math.sqrt(total_rows)
    pre_whole = lax.psum(jnp.dot(inputs, w_in, preferred_element_type=jnp.float32), "row")
    hidden = gelu_value(pre_whole).astype(jnp.bfloat16)
    block = hidden
    mixed = sum_at_owner(
        jnp.dot(block, w_out, preferred_element_type=jnp.float32), "col", 0
    ).astype(jnp.bfloat16)
    grads = lax.all_gather(cotangent[0], "col", axis=0, tiled=True)
    block = grads
    back_whole = lax.psum(
        lax.dot_general(
            block, w_out, (((1,), (1,)), ((), ())), preferred_element_type=jnp.float32
        ).astype(jnp.bfloat16),
        "row",
    ).astype(jnp.float32)
    slope = (back_whole * gelu_slope(pre_whole)).astype(jnp.bfloat16)
    grad_first = (
        lax.dot_general(inputs, slope, (((0,), (0,)), ((), ())), preferred_element_type=jnp.float32)
        * norm_factor
    )
    grad_second = (
        lax.dot_general(hidden, grads, (((0,), (0,)), ((), ())), preferred_element_type=jnp.float32)
        * norm_factor
    )
    moved_first = (
        momentum_decay * moment_in[0].astype(jnp.float32) + (1.0 - momentum_decay) * grad_first
    )
    moved_second = (
        momentum_decay * moment_out[0].astype(jnp.float32) + (1.0 - momentum_decay) * grad_second
    )
    vote_first = jnp.tanh(moved_first / vote_scale).astype(jnp.bfloat16)
    vote_second = jnp.tanh(moved_second / vote_scale).astype(jnp.bfloat16)
    tally_first, tally_second = (
        lax.psum(vote_first, "rep").astype(jnp.float32),
        lax.psum(vote_second, "rep").astype(jnp.float32),
    )
    return (mixed[None], tally_first.astype(jnp.bfloat16), tally_second.astype(jnp.bfloat16))


def solution(mesh):
    in_specs = (
        P("rep", "col", "row"),
        P("rep", "col", "row"),
        P("row", "col"),
        P("col", "row"),
        P("rep", "row", "col"),
        P("rep", "col", "row"),
    )
    out_specs = (P("rep", "col", "row"), P("row", "col"), P("col", "row"))
    return jax.shard_map(shards, mesh=mesh, in_specs=in_specs, out_specs=out_specs, check_vma=False)
```

profile of v0, /device:TPU:1, one launch (start us, length us, event | category | flops | bytes accessed | tf_op | source)
XLA Modules:
  0.0 338.2 jit_solution(2649844550422343762)
XLA Ops:
  7.2 0.0 all-reduce.5.cloned.1.call-start
  7.2 1.0 broadcast_in_dim.4
  8.2 22.4 %all_to_all.10 = bf16[8,64,384]{2,1,0:T(8,128)(2,1)S(1)} all-to-all(bf16[8,64,384]{2,1,0:T(8,128)(2,1)S(1)} %broadcast_in_dim.4), channel_id=1, replica_groups=mesh['row'=16,'col'=8,'rep'=2] {'col'}, dimensions={0} | all-to-all | bytes 786432 | tf_op jit(solution)/shard_map/all_to_all | solution.py:19
  30.6 6.1 %fusion.20 = f32[512,3072]{1,0:T(8,128)} fusion(bf16[512,384]{1,0:T(8,128)(2,1)S(1)} %bitcast.36, bf16[384,3072]{1,0:T(8,128)(2,1)} %param.8), kind=kOutput, calls=%fused_computation.26 | convolution fusion | flops 1207959552 | bytes 9043968 | tf_op jit(solution)/shard_map/dot_general | solution.py:51
  36.7 0.0 all-reduce.5.cloned.1.call-update
  36.7 0.0 all-reduce.7.cloned.1.call-start
  36.8 0.7 copy-done.2
  37.5 20.5 %all-gather = bf16[1,512,384]{2,1,0:T(8,128)(2,1)S(1)} all-gather(bf16[1,64,384]{2,1,0:T(8,128)(2,1)S(1)} %copy-done.2), channel_id=2, replica_groups=mesh['row'=16,'col'=8,'rep'=2] {'col'}, dimensions={1}, use_global_device_ids=true | all-gather | bytes 442368 | tf_op jit(solution)/shard_map/all_gather | solution.py:57
  58.0 3.5 %convolution_convert_fusion = bf16[512,3072]{1,0:T(8,128)(2,1)} fusion(bf16[3072,384]{1,0:T(8,128)(2,1)S(1)} %copy-done, bf16[1,512,384]{2,1,0:T(8,128)(2,1)S(1)} %all-gather), kind=kOutput, calls=%fused_computation.17 | convolution fusion | flops 1209532416 | bytes 5898240 | tf_op jit(solution)/shard_map/dot_general | solution.py:60
  61.4 0.0 all-reduce.7.cloned.1.call-update
  61.5 0.0 all-reduce.9.cloned.1.call-start
  61.5 4.3 %copy.9 = bf16[1,384,3072]{1,2,0:T(8,128)(2,1)} copy(bf16[1,384,3072]{2,1,0:T(8,128)(2,1)} %param.10) | data formatting | bytes 4718592 | tf_op args[4]
  65.8 101.0 %all-reduce.5.cloned.1.call-done = f32[512,3072]{1,0:T(8,128)} async-done(((f32[512,3072]{1,0:T(8,128)}), f32[512,3072]{1,0:T(8,128)}) %all-reduce.5.cloned.1.call-update) | async-done | bytes 6291472 | tf_op jit(solution)/shard_map/psum | solution.py:51
  166.8 3.6 %multiply_convert_fusion = bf16[512,3072]{1,0:T(8,128)(2,1)S(1)} fusion(f32[512,3072]{1,0:T(8,128)} %all-reduce.5.cloned.1.call-done), kind=kLoop, calls=%fused_computation.7 | loop fusion | flops 7864320 | bytes 9437184 | tf_op jit(solution)/shard_map/convert_element_type | solution.py:52
  170.4 1.7 copy-done.1
  172.1 4.0 %fusion.8 = bf16[3072,384]{1,0:T(8,128)(2,1)} fusion(bf16[1,3072,384]{2,1,0:T(8,128)(2,1)S(1)} %copy-done.3, bf16[512,3072]{1,0:T(8,128)(2,1)S(1)} %multiply_convert_fusion, bf16[1,512,384]{2,1,0:T(8,128)(2,1)S(1)} %all-gather), kind=kOutput, calls=%fused_computation.12 | convolution fusion | flops 1215037440 | bytes 8257536 | tf_op jit(solution)/shard_map/dot_general | solution.py:71
  176.1 99.6 %all-reduce.7.cloned.1.call-done = bf16[512,3072]{1,0:T(8,128)(2,1)} async-done(((bf16[512,3072]{1,0:T(8,128)(2,1)}), bf16[512,3072]{1,0:T(8,128)(2,1)}) %all-reduce.7.cloned.1.call-update) | async-done | bytes 3145744 | tf_op jit(solution)/shard_map/psum | solution.py:59
  275.7 8.4 %fusion.11 = bf16[384,3072]{0,1:T(8,128)(2,1)} fusion(bf16[1,384,3072]{1,2,0:T(8,128)(2,1)} %copy.9, bf16[512,384]{1,0:T(8,128)(2,1)S(1)} %bitcast.37, f32[512,3072]{1,0:T(8,128)} %all-reduce.5.cloned.1.call-done, bf16[512,3072]{1,0:T(8,128)(2,1)} %all-reduce.7.cloned.1.call-done), kind=kOutput, calls=%fused_computation.16 | convolution fusion | flops 1232338944 | bytes 14548992 | tf_op jit(solution)/shard_map/dot_general | solution.py:67
  284.1 3.7 %fusion.21 = f32[512,384]{1,0:T(8,128)S(1)} fusion(bf16[512,3072]{1,0:T(8,128)(2,1)} %copy-done.1, bf16[3072,384]{1,0:T(8,128)(2,1)S(1)} %copy-done), kind=kOutput, calls=%fused_computation.27 | convolution fusion | flops 1207959552 | bytes 6291456 | tf_op jit(solution)/shard_map/dot_general | solution.py:55
  287.8 27.9 %all_to_all.11 = f32[8,64,384]{2,1,0:T(8,128)S(1)} all-to-all(f32[8,64,384]{2,1,0:T(8,128)S(1)} %bitcast.38), channel_id=1, replica_groups=mesh['row'=16,'col'=8,'rep'=2] {'col'}, dimensions={0} | all-to-all | bytes 1572864 | tf_op jit(solution)/shard_map/all_to_all | solution.py:33
  315.7 0.7 reduce_sum.9
  316.4 7.7 %all-reduce.9.cloned.1.call-done = (bf16[384,3072]{0,1:T(8,128)(2,1)}, bf16[3072,384]{1,0:T(8,128)(2,1)}) async-done(((bf16[384,3072]{0,1:T(8,128)(2,1)}, bf16[3072,384]{1,0:T(8,128)(2,1)}), (bf16[384,3072]{0,1:T(8,128)(2,1)}, bf16[3072,384]{1,0:T(8,128)(2,1)})) %all-reduce.9.cloned.1.call-update) | async-done | bytes 4718608 | tf_op jit(solution)/shard_map/psum | solution.py:83
  324.1 4.3 %copy.10 = bf16[384,3072]{1,0:T(8,128)(2,1)} copy(bf16[384,3072]{0,1:T(8,128)(2,1)} %get-tuple-element.6) | data formatting | bytes 4718592
  328.4 3.3 copy.15
  (7 shorter events, 0.0 us)
Async XLA Ops:
  7.2 50.8 %copy-start = (bf16[3072,384]{1,0:T(8,128)(2,1)S(1)}, bf16[3072,384]{1,0:T(8,128)(2,1)}, u32[]{:S(2)}) copy-start(bf16[3072,384]{1,0:T(8,128)(2,1)} %param.9) | copy-start | bytes 7077892
  7.2 159.7 %all-reduce.5.cloned.1.call-start = ((), (), s32[]{:S(2)}) async-start(), calls=%async_computation.2 | async-start | bytes 12582912 | tf_op jit(solution)/shard_map/psum | solution.py:51
  36.7 0.8 copy-start.2
  36.7 239.0 %all-reduce.7.cloned.1.call-start = ((), (), s32[]{:S(2)}) async-start(), calls=%async_computation.3 | async-start | bytes 6291456 | tf_op jit(solution)/shard_map/psum | solution.py:59
  61.5 262.7 %all-reduce.9.cloned.1.call-start = ((), (), s32[]{:S(2)}) async-start(), calls=%async_computation.4 | async-start | bytes 9437184 | tf_op jit(solution)/shard_map/psum | solution.py:83
  166.8 5.3 %copy-start.3 = (bf16[1,3072,384]{2,1,0:T(8,128)(2,1)S(1)}, bf16[1,3072,384]{2,1,0:T(8,128)(2,1)}, u32[]{:S(2)}) copy-start(bf16[1,3072,384]{2,1,0:T(8,128)(2,1)} %param.11) | copy-start | bytes 7077892
  170.4 1.7 copy-start.1
Sparse Core Ops, SparseCore 0:
  36.9 129.9 all-reduce.4
  170.2 105.4 all-reduce.6
  284.2 39.8 all-reduce.8
where the time goes:
time: 339 us; the launch traced here: 338 us
  waiting for transfers between devices  208 us (61%)
  blocking collectives  70.8 us (21%)
  matrix products  25.6 us (8%)
  local copies, waits for them, and re-layouts  15.3 us (5%)
  between operations  13.8 us (4%)
  other arithmetic  4.23 us (1%)
    psum x1, waiting for transfers between devices, shards(): lax.psum(jnp.dot(inputs, w_in, preferred_element_type=jnp.float32), 'row')  101 us
    psum x1, waiting for transfers between devices, shards(): lax.psum(lax.dot_general(block, w_out, (((1,), (1,)), ((), ())), preferre...  99.6 us
    all_to_all x1, blocking collectives, sum_at_owner(): lax.all_to_all(blocks, axis, split_axis=0, concat_axis=0, tiled=True)  27.9 us
    all_to_all x1, blocking collectives, sent_to_all(): return lax.all_to_all(copies, axis, split_axis=0, concat_axis=0, tiled=True)  22.4 us
    all_gather x1, blocking collectives, shards(): grads = lax.all_gather(cotangent[0], 'col', axis=0, tiled=True)  20.5 us
    unnamed x11, local copies, waits for them, and re-layouts  14.3 us
    dot_general x1, matrix products, shards(): lax.dot_general(inputs, slope, (((0,), (0,)), ((), ())), preferred_elemen...  8.39 us
    psum x1, waiting for transfers between devices, shards(): lax.psum(vote_first, 'rep').astype(jnp.float32)  7.74 us
  transfers between devices with their start and end apart: 3, of which 3 were waited for; matrix products, arithmetic and copies ran while one was open for 6% of the time, Pallas kernels for 0%

commit v1 on v0

--- a/solution.py
+++ b/solution.py
@@ -6,6 +6,14 @@
 
 momentum_decay = 0.9
 vote_scale = 0.3
+
+
+def wrap_surface(tile_in, dim_at):
+    tile_in = jnp.moveaxis(tile_in, 0, dim_at)
+    part_next = tile_in.shape
+    return tile_in.reshape(
+        *part_next[:dim_at], part_next[dim_at] * part_next[dim_at + 1], *part_next[dim_at + 2 :]
+    )
 
 
 def joined_along(blocks, dim):
@@ -45,6 +53,27 @@
 
 
 def shards(patches, cotangent, w_in, w_out, moment_in, moment_out):
+
+    def wires_pass(across, dim_i, sample):
+        parts_n = lax.axis_size(across)
+        samples = [(j, (j + 1) % parts_n) for j in range(parts_n)]
+        history = [(c, d) for d, c in samples]
+        upper, g_now = ([], [])
+        t = 0
+        while t < parts_n - 1:
+            if t % 2 == 0:
+                upper.append(lax.ppermute(upper[-1] if upper else sample, across, perm=samples))
+            else:
+                small = lax.ppermute(g_now[-1] if g_now else sample, across, perm=history)
+                g_now.append(small)
+            t += 1
+        spare = jnp.stack([*upper[::-1], sample, *g_now])
+        b_now = lax.axis_index(across)
+        high = len(upper)
+        arr_out = b_now - high
+        spare = spare[(jnp.arange(parts_n) - arr_out) % parts_n]
+        return wrap_surface(spare, dim_i)
+
     inputs = gather_directly(patches[0], "col", 0)
     total_rows = inputs.shape[0]
     norm_factor = 1.0 / math.sqrt(total_rows)
@@ -54,7 +83,7 @@
     mixed = sum_at_owner(
         jnp.dot(block, w_out, preferred_element_type=jnp.float32), "col", 0
     ).astype(jnp.bfloat16)
-    grads = lax.all_gather(cotangent[0], "col", axis=0, tiled=True)
+    grads = wires_pass("col", 0, cotangent[0])
     block = grads
     back_whole = lax.psum(
         lax.dot_general(

time: 339 us -> 339 us (level)
  blocking collectives: 70.8 us -> 50.3 us
  waiting for transfers between devices: 208 us -> 219 us
  starting transfers between devices: 0.12 us -> 9.01 us
    all_gather x1 -> x0, blocking collectives: 20.5 us -> none  [shards(): grads = lax.all_gather(cotangent[0], 'col', axis=0, tiled=True)]
    ppermute x0 -> x7, waiting for transfers between devices: none -> 8.96 us  [the longest x4 8.95 us: wires_pass(): lax.ppermute(upper[-1] if upper else sample, across, perm=samples)]
    ppermute x0 -> x7, starting transfers between devices: none -> 8.71 us  [the longest x3 8.36 us: wires_pass(): small = lax.ppermute(g_now[-1] if g_now else sample, across, perm=history)]
    unnamed x11 -> x18, local copies, waits for them, and re-layouts: 14.3 us -> 14.4 us
  transfers between devices with their start and end apart: 3 -> 10, of which waited for: 3 -> 7; matrix products, arithmetic and copies ran while one was open for 6% -> 6% of each run, Pallas kernels for 0% -> 0%
where the time goes in v1:
time: 339 us; the launch traced here: 338 us
  waiting for transfers between devices  219 us (65%)
  blocking collectives  50.3 us (15%)
  matrix products  25.6 us (8%)
  local copies, waits for them, and re-layouts  16.1 us (5%)
  between operations  13.9 us (4%)
  starting transfers between devices  9.01 us (3%)
  other arithmetic  4.25 us (1%)
    psum x1, waiting for transfers between devices, shards(): lax.psum(jnp.dot(inputs, w_in, preferred_element_type=jnp.float32), 'row')  103 us
    psum x1, waiting for transfers between devices, shards(): lax.psum(lax.dot_general(block, w_out, (((1,), (1,)), ((), ())), preferre...  99.6 us
    all_to_all x1, blocking collectives, sum_at_owner(): lax.all_to_all(blocks, axis, split_axis=0, concat_axis=0, tiled=True)  27.9 us
    all_to_all x1, blocking collectives, sent_to_all(): return lax.all_to_all(copies, axis, split_axis=0, concat_axis=0, tiled=True)  22.4 us
    unnamed x18, local copies, waits for them, and re-layouts  14.4 us
    ppermute x4, waiting for transfers between devices, wires_pass(): lax.ppermute(upper[-1] if upper else sample, across, perm=samples)  8.95 us
    dot_general x1, matrix products, shards(): lax.dot_general(inputs, slope, (((0,), (0,)), ((), ())), preferred_elemen...  8.39 us
    ppermute x3, starting transfers between devices, wires_pass(): small = lax.ppermute(g_now[-1] if g_now else sample, across, perm=history)  8.36 us
  transfers between devices with their start and end apart: 10, of which 7 were waited for; matrix products, arithmetic and copies ran while one was open for 6% of the time, Pallas kernels for 0%

profile of v1, /device:TPU:1, one launch (start us, length us, event | category | flops | bytes accessed | tf_op | source)
XLA Modules:
  0.0 338.3 jit_solution(12596646234505062026)
XLA Ops:
  7.2 1.0 broadcast_in_dim.2
  8.2 22.4 %all_to_all.10 = bf16[8,64,384]{2,1,0:T(8,128)(2,1)S(1)} all-to-all(bf16[8,64,384]{2,1,0:T(8,128)(2,1)S(1)} %broadcast_in_dim.2), channel_id=1, replica_groups=mesh['row'=16,'col'=8,'rep'=2] {'col'}, dimensions={0} | all-to-all | bytes 786432 | tf_op jit(solution)/shard_map/all_to_all | solution.py:27
  30.6 6.1 %fusion.20 = f32[512,3072]{1,0:T(8,128)} fusion(bf16[512,384]{1,0:T(8,128)(2,1)S(1)} %bitcast.51, bf16[384,3072]{1,0:T(8,128)(2,1)} %param.8), kind=kOutput, calls=%fused_computation.40 | convolution fusion | flops 1207959552 | bytes 9043968 | tf_op jit(solution)/shard_map/dot_general | solution.py:80
  36.8 0.7 copy-done.2
  37.9 3.8 %collective-permute-done = bf16[64,384]{1,0:T(8,128)(2,1)S(1)} collective-permute-done((bf16[64,384]{1,0:T(8,128)(2,1)S(1)}, bf16[64,384]{1,0:T(8,128)(2,1)S(1)}, u32[]{:S(2)}, u32[]{:S(2)}) %collective-permute-start) | collective-permute-done | bytes 49184 | tf_op jit(solution)/shard_map/ppermute | solution.py:65
  41.7 2.7 collective-permute-start.4
  44.3 1.5 collective-permute-done.1
  45.8 2.7 collective-permute-start.5
  48.6 1.8 collective-permute-done.2
  50.4 2.9 collective-permute-start.6
  53.4 1.9 collective-permute-done.3
  56.0 3.5 %convolution_convert_fusion = bf16[512,3072]{1,0:T(8,128)(2,1)} fusion(bf16[512,384]{1,0:T(8,128)(2,1)S(1)} %bitcast.54, bf16[3072,384]{1,0:T(8,128)(2,1)S(1)} %copy-done), kind=kOutput, calls=%fused_computation.18 | convolution fusion | flops 1209532416 | bytes 5898240 | tf_op jit(solution)/shard_map/dot_general | solution.py:89
  59.8 4.3 %copy.9 = bf16[1,384,3072]{1,2,0:T(8,128)(2,1)} copy(bf16[1,384,3072]{2,1,0:T(8,128)(2,1)} %param.10) | data formatting | bytes 4718592 | tf_op args[4]
  64.1 102.8 %all-reduce.5.cloned.1.call-done = f32[512,3072]{1,0:T(8,128)} async-done(((f32[512,3072]{1,0:T(8,128)}), f32[512,3072]{1,0:T(8,128)}) %all-reduce.5.cloned.1.call-update) | async-done | bytes 6291472 | tf_op jit(solution)/shard_map/psum | solution.py:80
  166.9 3.6 %multiply_convert_fusion = bf16[512,3072]{1,0:T(8,128)(2,1)S(1)} fusion(f32[512,3072]{1,0:T(8,128)} %all-reduce.5.cloned.1.call-done), kind=kLoop, calls=%fused_computation.8 | loop fusion | flops 7864320 | bytes 9437184 | tf_op jit(solution)/shard_map/convert_element_type | solution.py:81
  170.5 1.7 copy-done.1
  172.2 4.0 %fusion.8 = bf16[3072,384]{1,0:T(8,128)(2,1)} fusion(bf16[1,3072,384]{2,1,0:T(8,128)(2,1)S(1)} %copy-done.3, bf16[512,3072]{1,0:T(8,128)(2,1)S(1)} %multiply_convert_fusion, bf16[512,384]{1,0:T(8,128)(2,1)S(1)} %bitcast.55), kind=kOutput, calls=%fused_computation.13 | convolution fusion | flops 1215037440 | bytes 8257536 | tf_op jit(solution)/shard_map/dot_general | solution.py:100
  176.1 99.6 %all-reduce.7.cloned.1.call-done = bf16[512,3072]{1,0:T(8,128)(2,1)} async-done(((bf16[512,3072]{1,0:T(8,128)(2,1)}), bf16[512,3072]{1,0:T(8,128)(2,1)}) %all-reduce.7.cloned.1.call-update) | async-done | bytes 3145744 | tf_op jit(solution)/shard_map/psum | solution.py:88
  275.7 8.4 %fusion.11 = bf16[384,3072]{0,1:T(8,128)(2,1)} fusion(bf16[1,384,3072]{1,2,0:T(8,128)(2,1)} %copy.9, bf16[512,384]{1,0:T(8,128)(2,1)S(1)} %bitcast.52, f32[512,3072]{1,0:T(8,128)} %all-reduce.5.cloned.1.call-done, bf16[512,3072]{1,0:T(8,128)(2,1)} %all-reduce.7.cloned.1.call-done), kind=kOutput, calls=%fused_computation.17 | convolution fusion | flops 1232338944 | bytes 14548992 | tf_op jit(solution)/shard_map/dot_general | solution.py:96
  284.2 3.7 %fusion.21 = f32[512,384]{1,0:T(8,128)S(1)} fusion(bf16[512,3072]{1,0:T(8,128)(2,1)} %copy-done.1, bf16[3072,384]{1,0:T(8,128)(2,1)S(1)} %copy-done), kind=kOutput, calls=%fused_computation.41 | convolution fusion | flops 1207959552 | bytes 6291456 | tf_op jit(solution)/shard_map/dot_general | solution.py:84
  287.8 27.9 %all_to_all.11 = f32[8,64,384]{2,1,0:T(8,128)S(1)} all-to-all(f32[8,64,384]{2,1,0:T(8,128)S(1)} %bitcast.53), channel_id=1, replica_groups=mesh['row'=16,'col'=8,'rep'=2] {'col'}, dimensions={0} | all-to-all | bytes 1572864 | tf_op jit(solution)/shard_map/all_to_all | solution.py:41
  316.4 7.7 %all-reduce.9.cloned.1.call-done = (bf16[384,3072]{0,1:T(8,128)(2,1)}, bf16[3072,384]{1,0:T(8,128)(2,1)}) async-done(((bf16[384,3072]{0,1:T(8,128)(2,1)}, bf16[3072,384]{1,0:T(8,128)(2,1)}), (bf16[384,3072]{0,1:T(8,128)(2,1)}, bf16[3072,384]{1,0:T(8,128)(2,1)})) %all-reduce.9.cloned.1.call-update) | async-done | bytes 4718608 | tf_op jit(solution)/shard_map/psum | solution.py:112
  324.2 4.3 %copy.10 = bf16[384,3072]{1,0:T(8,128)(2,1)} copy(bf16[384,3072]{0,1:T(8,128)(2,1)} %get-tuple-element.6) | data formatting | bytes 4718592
  328.4 3.3 copy.22
  (31 shorter events, 2.1 us)
Async XLA Ops:
  7.2 48.8 %copy-start = (bf16[3072,384]{1,0:T(8,128)(2,1)S(1)}, bf16[3072,384]{1,0:T(8,128)(2,1)}, u32[]{:S(2)}) copy-start(bf16[3072,384]{1,0:T(8,128)(2,1)} %param.9) | copy-start | bytes 7077892
  7.2 159.7 %all-reduce.5.cloned.1.call-start = ((), (), s32[]{:S(2)}) async-start(), calls=%async_computation.2 | async-start | bytes 12582912 | tf_op jit(solution)/shard_map/psum | solution.py:80
  36.7 0.8 copy-start.2
  36.7 239.0 %all-reduce.7.cloned.1.call-start = ((), (), s32[]{:S(2)}) async-start(), calls=%async_computation.3 | async-start | bytes 6291456 | tf_op jit(solution)/shard_map/psum | solution.py:88
  37.5 4.2 %collective-permute-start = (bf16[64,384]{1,0:T(8,128)(2,1)S(1)}, bf16[64,384]{1,0:T(8,128)(2,1)S(1)}, u32[]{:S(2)}, u32[]{:S(2)}) collective-permute-start(bf16[64,384]{1,0:T(8,128)(2,1)S(1)} %bitcast.58), channel_id=1, source_target_pairs={{0,2},{2,4},{4,6},{6,8},{8,10},{10,12},{12,14},{14,0},{1,3},{3,5},... | collective-permute-start | bytes 147464 | tf_op jit(solution)/shard_map/ppermute | solution.py:65
  41.7 4.2 %collective-permute-start.1 = (bf16[64,384]{1,0:T(8,128)(2,1)S(1)}, bf16[64,384]{1,0:T(8,128)(2,1)S(1)}, u32[]{:S(2)}, u32[]{:S(2)}) collective-permute-start(bf16[64,384]{1,0:T(8,128)(2,1)S(1)} %collective-permute-done), channel_id=1, source_target_pairs={{0,2},{2,4},{4,6},{6,8},{8,10},{10,12},{12,14},{14,0},{1,3},{3,5},... | collective-permute-start | bytes 147464 | tf_op jit(solution)/shard_map/ppermute | solution.py:65
  41.7 4.2 %collective-permute-start.4 = (bf16[64,384]{1,0:T(8,128)(2,1)S(1)}, bf16[64,384]{1,0:T(8,128)(2,1)S(1)}, u32[]{:S(2)}, u32[]{:S(2)}) collective-permute-start(bf16[64,384]{1,0:T(8,128)(2,1)S(1)} %bitcast.59), channel_id=1, source_target_pairs={{2,0},{4,2},{6,4},{8,6},{10,8},{12,10},{14,12},{0,14},{3,1},{5,3},... | collective-permute-start | bytes 147464 | tf_op jit(solution)/shard_map/ppermute | solution.py:67
  45.8 4.6 %collective-permute-start.2 = (bf16[64,384]{1,0:T(8,128)(2,1)S(1)}, bf16[64,384]{1,0:T(8,128)(2,1)S(1)}, u32[]{:S(2)}, u32[]{:S(2)}) collective-permute-start(bf16[64,384]{1,0:T(8,128)(2,1)S(1)} %collective-permute-done.1), channel_id=1, source_target_pairs={{0,2},{2,4},{4,6},{6,8},{8,10},{10,12},{12,14},{14,0},{1,3},{3,5},... | collective-permute-start | bytes 147464 | tf_op jit(solution)/shard_map/ppermute | solution.py:65
  45.8 4.6 %collective-permute-start.5 = (bf16[64,384]{1,0:T(8,128)(2,1)S(1)}, bf16[64,384]{1,0:T(8,128)(2,1)S(1)}, u32[]{:S(2)}, u32[]{:S(2)}) collective-permute-start(bf16[64,384]{1,0:T(8,128)(2,1)S(1)} %collective-permute-done.4), channel_id=1, source_target_pairs={{2,0},{4,2},{6,4},{8,6},{10,8},{12,10},{14,12},{0,14},{3,1},{5,3},... | collective-permute-start | bytes 147464 | tf_op jit(solution)/shard_map/ppermute | solution.py:67
  50.4 4.8 %collective-permute-start.3 = (bf16[64,384]{1,0:T(8,128)(2,1)S(1)}, bf16[64,384]{1,0:T(8,128)(2,1)S(1)}, u32[]{:S(2)}, u32[]{:S(2)}) collective-permute-start(bf16[64,384]{1,0:T(8,128)(2,1)S(1)} %collective-permute-done.2), channel_id=1, source_target_pairs={{0,2},{2,4},{4,6},{6,8},{8,10},{10,12},{12,14},{14,0},{1,3},{3,5},... | collective-permute-start | bytes 147464 | tf_op jit(solution)/shard_map/ppermute | solution.py:65
  50.4 4.9 %collective-permute-start.6 = (bf16[64,384]{1,0:T(8,128)(2,1)S(1)}, bf16[64,384]{1,0:T(8,128)(2,1)S(1)}, u32[]{:S(2)}, u32[]{:S(2)}) collective-permute-start(bf16[64,384]{1,0:T(8,128)(2,1)S(1)} %collective-permute-done.5), channel_id=1, source_target_pairs={{2,0},{4,2},{6,4},{8,6},{10,8},{12,10},{14,12},{0,14},{3,1},{5,3},... | collective-permute-start | bytes 147464 | tf_op jit(solution)/shard_map/ppermute | solution.py:67
  59.5 264.6 %all-reduce.9.cloned.1.call-start = ((), (), s32[]{:S(2)}) async-start(), calls=%async_computation.4 | async-start | bytes 9437184 | tf_op jit(solution)/shard_map/psum | solution.py:112
  166.9 5.3 %copy-start.3 = (bf16[1,3072,384]{2,1,0:T(8,128)(2,1)S(1)}, bf16[1,3072,384]{2,1,0:T(8,128)(2,1)}, u32[]{:S(2)}) copy-start(bf16[1,3072,384]{2,1,0:T(8,128)(2,1)} %param.11) | copy-start | bytes 7077892
  170.5 1.7 copy-start.1
Sparse Core Ops, SparseCore 0:
  36.9 129.9 all-reduce.4
  170.2 105.4 all-reduce.6
  284.3 39.8 all-reduce.8
